TPU v7x, 32 devices: a whole 2x2x4 slice. The times are simulated.
32 devices in a mesh: gx: 4 (over y, x), gy: 4 (over z), gz: 2 (over core).
Axes of the slice: x: 2, y: 2, z: 4, core: 2. Of those that a mesh axis runs over, the one named last changes fastest.
Arguments:
- gas_pos: float32 [3, 4, 4, 2, 2048], P(None, 'gx', 'gy', 'gz'), may hold values from 0 to 1
- gas_mass: float32 [4, 4, 2, 2048], P('gx', 'gy', 'gz'), may hold values from 0.2 to 5
- source_pos: float32 [3, 4, 4, 2, 2048], P(None, 'gx', 'gy', 'gz'), may hold values from 0 to 1
- source_radius: float32 [4, 4, 2, 2048], P('gx', 'gy', 'gz'), may hold values from 0.25 to 1
- source_yield: float32 [2, 4, 4, 2, 2048], P(None, 'gx', 'gy', 'gz'), may hold values from 1 to 30
- source_momentum: float32 [3, 4, 4, 2, 2048], P(None, 'gx', 'gy', 'gz'), may hold values from -180 to 180
- source_tiles: int32 [4, 4, 2, 16, 8], P('gx', 'gy', 'gz'), may hold values from 0 to 431, as said below
- source_count: int32 [4, 4, 2], P('gx', 'gy', 'gz'), may hold values from 1 to 2048, as said below
Outputs:
- gas_gain: float32 [5, 4, 4, 2, 2048], P(None, 'gx', 'gy', 'gz')
Inputs may be any that keep to these rules, and one draw needn't show every extreme that they name: `source_tiles`: the 8 tiles of one block lie one in each of the 8 domains around one corner of the block's domain (that domain among them), in increasing order. Over all blocks of one domain, at most 8 distinct listed tiles lie in any one neighbouring slot. `source_count`: some domain holds 2048 live sources in every draw.
All inputs are finite; a program needn't handle non-finite values.
Results may differ from a plain program's by a relative error of at most 0.0003.
Values sent between devices are 32-bit elements; how exact they have to be, the bound alone decides.
A program may use at most 64 MiB of HBM per device.

v0:
```python
import functools
import math

import jax
import jax.numpy as jnp
from jax import lax
from jax.experimental import pallas as pl
from jax.experimental.pallas import tpu as pltpu
from jax.sharding import PartitionSpec as P


def kinds(count):
    return min(count, 3)


def kind_of(offset, count):
    if count >= 3:
        return offset + 1
    if count == 2:
        return jnp.abs(offset)
    return offset * 0


def own_kind(count):
    return 1 if count >= 3 else 0


def steps_of(count):
    if count >= 3:
        return ((0, -1), (2, 1))
    return ((1, 1),) if count == 2 else ()


MESH = pl.DeviceIdType.MESH
LIMIT = 24 * 1024 * 1024


def shifted(axis, count, step):
    return lax.rem(lax.axis_index(axis) + step + count, count)


def columns_of(sizes):
    nx, ny, _ = sizes
    choices_x = steps_of(nx) + ((own_kind(nx), 0),)
    choices_y = ((own_kind(ny), 0),) + steps_of(ny)
    return [
        ((i, j), {"gx": shifted("gx", nx, dx), "gy": shifted("gy", ny, dy)})
        for i, dx in choices_x
        for j, dy in choices_y
        if dx or dy
    ]


def cores_of(sizes):
    return [(k, {"gz": shifted("gz", sizes[2], dz)}) for k, dz in steps_of(sizes[2])]


def greet(sizes):
    barrier = pltpu.get_barrier_semaphore()
    peers = columns_of(sizes) + cores_of(sizes)
    for _, device in peers:
        pl.semaphore_signal(barrier, inc=1, device_id=device, device_id_type=MESH)
    if peers:
        pl.semaphore_wait(barrier, len(peers))


def facing(kind, count):
    return 2 - kind if count >= 3 else kind


def spread_kernel(sizes, pos, mass, near, local_sem, send_sem, recv_sem):
    nx, ny, nz = sizes
    own = tuple(own_kind(n) for n in sizes)

    def place(i, j, k):
        return (i * kinds(ny) + j) * kinds(nz) + k

    home = place(*own)
    first = pltpu.make_async_copy(pos, near.at[home, pl.ds(0, 3)], local_sem.at[0])
    second = pltpu.make_async_copy(mass, near.at[home, pl.ds(3, 1)], local_sem.at[1])
    first.start()
    second.start()
    greet(sizes)
    first.wait()
    second.wait()
    copies = {}

    def send(slot, there, device):
        target = place(*there)
        copy = pltpu.make_async_remote_copy(
            src_ref=near.at[place(*slot)],
            dst_ref=near.at[target],
            send_sem=send_sem.at[target],
            recv_sem=recv_sem.at[target],
            device_id=device,
            device_id_type=MESH,
        )
        copy.start()
        copies[there] = copy

    def to_cores(i, j):
        for k, device in cores_of(sizes):
            send((i, j, own[2]), (i, j, facing(k, nz)), device)

    columns = columns_of(sizes)
    for (i, j), device in columns:
        send(own, (facing(i, nx), facing(j, ny), own[2]), device)
    to_cores(own[0], own[1])
    across = [at for at, _ in columns if at[0] != own[0]]
    along = [at for at, _ in columns if at[0] == own[0]]
    for i, j in along + across:
        copies[i, j, own[2]].wait_recv()
        to_cores(i, j)
    for i, j in [own[:2]] + along + across:
        for k, _ in steps_of(nz):
            copies[i, j, k].wait_recv()
    for copy in copies.values():
        copy.wait_send()


def gather_kernel(sizes, moved, out, part, got_z, got, send_z, recv_z, send_sem, recv_sem):
    nx, ny, nz = sizes
    own = tuple(own_kind(n) for n in sizes)

    def place(i, j, k):
        return (i * kinds(ny) + j) * kinds(nz) + k

    greet(sizes)
    copies = []

    def send(src, dst, send_at, recv_at, device):
        copy = pltpu.make_async_remote_copy(
            src_ref=src, dst_ref=dst, send_sem=send_at, recv_sem=recv_at, device_id=device, device_id_type=MESH
        )
        copy.start()
        copies.append(copy)
        return copy

    columns = columns_of(sizes)
    order = [at for at, _ in columns] + [own[:2]]
    along_z, arriving = {}, {}
    for i, j in order:
        for k, device in cores_of(sizes):
            at = place(i, j, k)
            along_z[i, j, k] = send(moved.at[at], got_z.at[at], send_z.at[at], recv_z.at[at], device)

    def send_part(index):
        (i, j), device = columns[index]
        at = i * kinds(ny) + j
        arriving[at] = send(part.at[at], got.at[at], send_sem.at[at], recv_sem.at[at], device)

    for index, (i, j) in enumerate(order):
        total = moved[place(i, j, own[2])]
        for k, _ in steps_of(nz):
            along_z[i, j, k].wait_recv()
            total = total + got_z[place(i, j, k)]
        if index < len(columns):
            part[i * kinds(ny) + j] = total
        if index:
            send_part(index - 1)
    for at in reversed(list(arriving)):
        arriving[at].wait_recv()
        total = total + got[at]
    out[...] = total
    for copy in copies:
        copy.wait_send()


def split3(value):
    first = value.astype(jnp.bfloat16).astype(jnp.float32)
    rest = value - first
    second = rest.astype(jnp.bfloat16).astype(jnp.float32)
    return first, second, rest - second


def rows_of(rows):
    at = lax.broadcasted_iota(jnp.int32, (8, 128), 0)
    out = jnp.zeros((8, 128), jnp.float32)
    for i, row in enumerate(rows):
        out = jnp.where(at == i, row, out)
    return out


def deposit_kernel(sizes, tiles_each, unroll, table, count, near, pos, radius, yields, momentum, out, acc):
    blocks, listed = pos.shape[1], table.shape[0]
    slots = near.shape[0]
    nx, ny, nz = sizes
    acc[...] = jnp.zeros_like(acc)
    live_count = count[0]
    lane = lax.broadcasted_iota(jnp.int32, (1, 128), 1)

    def one_block(b):
        row = pl.ds(b, 1)
        r = radius[row, :]
        inv = 1.0 / (r * r)
        sx, sy, sz = (pos[k, row, :] - 0.5 for k in range(3))
        left = rows_of(
            [-2.0 * inv * sx, -2.0 * inv * sy, -2.0 * inv * sz, inv, 1.0 + inv * (sx * sx + sy * sy + sz * sz)]
        )
        a1, a2, a3 = split3(left)
        lhs = jnp.concatenate([a1, a1, a2, a2, a1, a3], axis=0).T.astype(jnp.bfloat16)
        norm_acc = jnp.zeros((128, 128), jnp.float32)
        high, low, places = [], [], []
        for j in range(listed):
            tile_id = table[j, b]
            slot, tile = tile_id // tiles_each, tile_id % tiles_each
            a, bb, c = slot // 9 - 1, slot // 3 % 3 - 1, slot % 3 - 1
            place = (kind_of(a, nx) * kinds(ny) + kind_of(bb, ny)) * kinds(nz) + kind_of(c, nz)
            places.append(place * tiles_each + tile)
            at = pl.ds(tile, 1)
            gx = near[place, 0, at, :] + (a.astype(jnp.float32) - 0.5)
            gy = near[place, 1, at, :] + (bb.astype(jnp.float32) - 0.5)
            gz = near[place, 2, at, :] + (c.astype(jnp.float32) - 0.5)
            mass = near[place, 3, at, :]
            b1, b2, b3 = split3(rows_of([gx, gy, gz, gx * gx + gy * gy + gz * gz, jnp.ones_like(gx)]))
            rhs = jnp.concatenate([b1, b2, b1, b2, b3, b1], axis=0).astype(jnp.bfloat16)
            u = jnp.dot(lhs, rhs, preferred_element_type=jnp.float32)
            w = 1.0 / (u * u)
            norm_acc = norm_acc + w * mass
            w1 = w.astype(jnp.bfloat16)
            high.append(w1)
            low.append((w - w1.astype(jnp.float32)).astype(jnp.bfloat16))
        norm = jnp.sum(norm_acc.T, axis=0, keepdims=True)
        live = jnp.where(b * 128 + lane < live_count, 1.0, 0.0)
        scale = live / norm
        loads = rows_of(
            [yields[0, row, :], momentum[0, row, :], momentum[1, row, :], momentum[2, row, :], yields[1, row, :]]
        )
        c1, c2, c3 = split3(loads * scale)
        coef = jnp.concatenate([c1, c2, c3, jnp.zeros_like(c1)], axis=0).astype(jnp.bfloat16)
        for j in range(listed):
            hi = jnp.dot(coef, high[j], preferred_element_type=jnp.float32)
            lo = jnp.dot(coef[0:16], low[j], preferred_element_type=jnp.float32)
            moved = hi[0:8] + (hi[8:16] + (hi[16:24] + (lo[0:8] + lo[8:16])))
            start = pl.multiple_of(places[j] * 8, 8)
            acc[pl.ds(start, 8), :] = acc[pl.ds(start, 8), :] + moved

    def step(i, carry):
        for k in range(unroll):
            one_block(i * unroll + k)
        return carry

    used = jnp.minimum((live_count + 127) // 128, blocks)
    lax.fori_loop(0, (used + unroll - 1) // unroll, step, 0)
    for slot in range(slots):
        for q in range(5):
            out[slot, q] = acc[pl.ds(slot * tiles_each * 8 + q, tiles_each, stride=8), :]


def local(sizes, gas_pos, gas_mass, source_pos, source_radius, source_yield, source_momentum, source_tiles, source_count):
    gas_size = gas_pos.shape[-1]
    tiles = gas_size // 128
    blocks = source_pos.shape[-1] // 128
    listed = source_tiles.shape[-1]
    nx, ny, nz = sizes
    slots = kinds(nx) * kinds(ny) * kinds(nz)
    vmem = pl.BlockSpec(memory_space=pltpu.VMEM)
    near = pl.pallas_call(
        functools.partial(spread_kernel, sizes),
        out_shape=pltpu.VMEM((slots, 4, tiles, 128), jnp.float32),
        in_specs=[vmem, vmem],
        out_specs=vmem,
        scratch_shapes=[
            pltpu.SemaphoreType.DMA((2,)),
            pltpu.SemaphoreType.DMA((slots,)),
            pltpu.SemaphoreType.DMA((slots,)),
        ],
        compiler_params=pltpu.CompilerParams(collective_id=0, has_side_effects=True, vmem_limit_bytes=LIMIT),
    )(gas_pos.reshape(3, tiles, 128), gas_mass.reshape(1, tiles, 128))
    unroll = math.gcd(blocks, 4)
    smem = pl.BlockSpec(memory_space=pltpu.SMEM)
    moved = pl.pallas_call(
        functools.partial(deposit_kernel, sizes, tiles, unroll),
        out_shape=pltpu.VMEM((slots, 5, tiles, 128), jnp.float32),
        in_specs=[smem, smem] + [vmem] * 5,
        out_specs=vmem,
        scratch_shapes=[pltpu.VMEM((slots * tiles * 8, 128), jnp.float32)],
        compiler_params=pltpu.CompilerParams(vmem_limit_bytes=LIMIT),
    )(
        source_tiles.reshape(blocks, listed).T,
        source_count.reshape(1),
        near,
        source_pos.reshape(3, blocks, 128),
        source_radius.reshape(blocks, 128),
        source_yield.reshape(2, blocks, 128),
        source_momentum.reshape(3, blocks, 128),
    )
    piece = (5, tiles, 128)
    sides = kinds(nx) * kinds(ny)
    gain = pl.pallas_call(
        functools.partial(gather_kernel, sizes),
        out_shape=jax.ShapeDtypeStruct(piece, jnp.float32),
        in_specs=[vmem],
        out_specs=vmem,
        scratch_shapes=[
            pltpu.VMEM((sides, *piece), jnp.float32),
            pltpu.VMEM((slots, *piece), jnp.float32),
            pltpu.VMEM((sides, *piece), jnp.float32),
            pltpu.SemaphoreType.DMA((slots,)),
            pltpu.SemaphoreType.DMA((slots,)),
            pltpu.SemaphoreType.DMA((sides,)),
            pltpu.SemaphoreType.DMA((sides,)),
        ],
        compiler_params=pltpu.CompilerParams(collective_id=1, has_side_effects=True, vmem_limit_bytes=LIMIT),
    )(moved)
    return gain.reshape(5, 1, 1, 1, gas_size)


def solution(mesh):
    sizes = (mesh.shape["gx"], mesh.shape["gy"], mesh.shape["gz"])
    in_specs = (
        P(None, "gx", "gy", "gz", None),
        P("gx", "gy", "gz", None),
        P(None, "gx", "gy", "gz", None),
        P("gx", "gy", "gz", None),
        P(None, "gx", "gy", "gz", None),
        P(None, "gx", "gy", "gz", None),
        P("gx", "gy", "gz", None, None),
        P("gx", "gy", "gz"),
    )
    out_specs = P(None, "gx", "gy", "gz", None)
    return jax.shard_map(
        functools.partial(local, sizes), mesh=mesh, in_specs=in_specs, out_specs=out_specs, check_vma=False
    )
```

profile of v0, /device:TPU:0, one launch (start us, length us, event | category | flops | bytes accessed | tf_op | source)
XLA Modules:
  0.0 37.5 jit_solution(15411207161180043788)
XLA Ops:
  0.7 0.0 copy-start.4
  0.7 0.7 %copy-done.4 = f32[1,1,1,2048]{3,2,1,0:T(1,128)S(1)} copy-done((f32[1,1,1,2048]{3,2,1,0:T(1,128)S(1)}, f32[1,1,1,2048]{3,2,1,0:T(1,128)}, u32[]{:S(2)}) %copy-start.4) | copy-done | bytes 8216
  1.4 0.0 copy-start
  1.4 0.7 %copy-done = f32[3,1,1,1,2048]{4,3,2,1,0:T(1,128)S(1)} copy-done((f32[3,1,1,1,2048]{4,3,2,1,0:T(1,128)S(1)}, f32[3,1,1,1,2048]{4,3,2,1,0:T(1,128)}, u32[]{:S(2)}) %copy-start) | copy-done | bytes 24600
  2.1 0.0 copy-start.1
  2.1 0.0 copy-start.2
  2.1 0.0 copy-start.3
  2.1 0.0 copy-start.5
  2.1 0.0 copy-start.6
  2.1 13.8 %shard_map.82.near = f32[18,4,16,128]{3,2,1,0:T(8,128)S(1)} custom-call(f32[3,16,128]{2,1,0:T(8,128)S(1)} %bitcast.13, f32[1,16,128]{2,1,0:T(8,128)S(1)} %bitcast.17), custom_call_target="tpu_custom_call" | custom-call | tf_op jit(solution)/shard_map/pallas_call | solution.py:258
  15.9 0.0 copy-done.1
  15.9 0.0 copy-done.2
  15.9 0.0 copy-done.3
  15.9 0.0 copy-done.5
  15.9 0.0 copy-done.6
  15.9 7.5 %shard_map.83.moved = f32[18,5,16,128]{3,2,1,0:T(8,128)S(1)} custom-call(s32[8,16]{1,0:T(8,128)S(1)} %bitcast.19, s32[1]{0:T(128)} %bitcast.11.count, f32[18,4,16,128]{3,2,1,0:T(8,128)S(1)} %shard_map.82.near, f32[3,16,128]{2,1,0:T(8,128)S(1)} %bitcast.14, f32[16,128]{1,0:T(8,128)S(1)} %bitcast.18, f32[2,16,128]{2,1,0:T(8,128)S(1)} %bitcast.16, ...), custom_call_target="tpu_custom_call" | custom-call | tf_op jit(solution)/shard_map/pallas_call | solution.py:272
  23.4 13.4 %shard_map.84 = f32[5,16,128]{2,1,0:T(8,128)S(1)} custom-call(f32[18,5,16,128]{3,2,1,0:T(8,128)S(1)} %shard_map.83.moved), custom_call_target="tpu_custom_call" | custom-call | tf_op jit(solution)/shard_map/pallas_call | solution.py:290
  36.9 0.6 %copy.13 = f32[5,1,1,1,2048]{4,3,2,1,0:T(1,128)} copy(f32[5,1,1,1,2048]{4,3,2,1,0:T(1,128)S(1)} %bitcast.12) | data formatting | bytes 81920
Async XLA Ops:
  0.7 0.7 %copy-start.4 = (f32[1,1,1,2048]{3,2,1,0:T(1,128)S(1)}, f32[1,1,1,2048]{3,2,1,0:T(1,128)}, u32[]{:S(2)}) copy-start(f32[1,1,1,2048]{3,2,1,0:T(1,128)} %param.9) | copy-start | bytes 24580
  1.4 0.7 %copy-start = (f32[3,1,1,1,2048]{4,3,2,1,0:T(1,128)S(1)}, f32[3,1,1,1,2048]{4,3,2,1,0:T(1,128)}, u32[]{:S(2)}) copy-start(f32[3,1,1,1,2048]{4,3,2,1,0:T(1,128)} %param.8) | copy-start | bytes 73732
  2.1 13.8 %copy-start.1 = (f32[3,1,1,1,2048]{4,3,2,1,0:T(1,128)S(1)}, f32[3,1,1,1,2048]{4,3,2,1,0:T(1,128)}, u32[]{:S(2)}) copy-start(f32[3,1,1,1,2048]{4,3,2,1,0:T(1,128)} %param.10) | copy-start | bytes 73732
  2.1 13.8 %copy-start.2 = (f32[3,1,1,1,2048]{4,3,2,1,0:T(1,128)S(1)}, f32[3,1,1,1,2048]{4,3,2,1,0:T(1,128)}, u32[]{:S(2)}) copy-start(f32[3,1,1,1,2048]{4,3,2,1,0:T(1,128)} %param.13) | copy-start | bytes 73732
  2.1 13.8 %copy-start.3 = (f32[2,1,1,1,2048]{4,3,2,1,0:T(1,128)S(1)}, f32[2,1,1,1,2048]{4,3,2,1,0:T(1,128)}, u32[]{:S(2)}) copy-start(f32[2,1,1,1,2048]{4,3,2,1,0:T(1,128)} %param.12) | copy-start | bytes 49156
  2.1 13.8 %copy-start.5 = (f32[1,1,1,2048]{3,2,1,0:T(1,128)S(1)}, f32[1,1,1,2048]{3,2,1,0:T(1,128)}, u32[]{:S(2)}) copy-start(f32[1,1,1,2048]{3,2,1,0:T(1,128)} %param.11) | copy-start | bytes 24580
  2.1 13.8 %copy-start.6 = (s32[1,1,1,16,8]{3,4,2,1,0:T(8,128)S(1)}, s32[1,1,1,16,8]{3,4,2,1,0:T(8,128)}, u32[]{:S(2)}) copy-start(s32[1,1,1,16,8]{3,4,2,1,0:T(8,128)} %param.14) | copy-start | bytes 1540
where the time goes:
time: 38.1 us; the launch traced here: 37.5 us
  Pallas kernels  34.7 us (91%)
  local copies, waits for them, and re-layouts  2.07 us (5%)
  between operations  0.74 us (2%)
    pallas_call x1, Pallas kernels, local(): pl.pallas_call(functools.partial(spread_kernel, sizes), out_shape=pltpu.V...  13.8 us
    pallas_call x1, Pallas kernels, local(): pl.pallas_call(functools.partial(gather_kernel, sizes), out_shape=jax.Sha...  13.4 us
    pallas_call x1, Pallas kernels, local(): pl.pallas_call(functools.partial(deposit_kernel, sizes, tiles, unroll), o...  7.52 us
    unnamed x15, local copies, waits for them, and re-layouts  2.07 us

commit v1 on v0

--- a/solution.py
+++ b/solution.py
@@ -118,7 +118,7 @@
         copy.wait_send()
 
 
-def gather_kernel(sizes, moved, out, part, got_z, got, send_z, recv_z, send_sem, recv_sem):
+def gather_kernel(sizes, moved, mass, out, part, got_z, got, send_z, recv_z, send_sem, recv_sem):
     nx, ny, nz = sizes
     own = tuple(own_kind(n) for n in sizes)
 
@@ -161,7 +161,7 @@
     for at in reversed(list(arriving)):
         arriving[at].wait_recv()
         total = total + got[at]
-    out[...] = total
+    out[...] = total / mass[...]
     for copy in copies:
         copy.wait_send()
 
@@ -173,78 +173,131 @@
     return first, second, rest - second
 
 
-def rows_of(rows):
-    at = lax.broadcasted_iota(jnp.int32, (8, 128), 0)
-    out = jnp.zeros((8, 128), jnp.float32)
-    for i, row in enumerate(rows):
-        out = jnp.where(at == i, row, out)
-    return out
-
-
-def deposit_kernel(sizes, tiles_each, unroll, table, count, near, pos, radius, yields, momentum, out, acc):
+def offsets():
+    return [(a, b, c) for a in (-1, 0, 1) for b in (-1, 0, 1) for c in (-1, 0, 1)]
+
+
+def kind_at(offset, count):
+    if count >= 3:
+        return offset + 1
+    return abs(offset) if count == 2 else 0
+
+
+def place_at(offset, sizes):
+    i, j, k = (kind_at(o, n) for o, n in zip(offset, sizes))
+    return (i * kinds(sizes[1]) + j) * kinds(sizes[2]) + k
+
+
+PARTS = 16
+
+
+def gas_features(gas, feat, slot, offset, tiles):
+    px, py, pz = (gas[k] + (offset[k] - 0.5) for k in range(3))
+    root = lax.rsqrt(gas[3])
+    square = (px * px + py * py + pz * pz) * root
+    rows = [split3(v) for v in (px * root, py * root, pz * root, square, root)]
+    base = slot * tiles * PARTS
+    for part in range(3):
+        for comp in range(5):
+            feat[pl.ds(base + part * 5 + comp, tiles, stride=PARTS), :] = rows[comp][part]
+    feat[pl.ds(base + 15, tiles, stride=PARTS), :] = jnp.zeros_like(px)
+
+
+def source_features(pos, radius, yields, momentum, rows, left, loads):
+    blocks = pos.shape[1]
+    r = radius[...]
+    inv = 1.0 / (r * r)
+    sx, sy, sz = (pos[k] - 0.5 for k in range(3))
+    comps = [-2.0 * inv * sx, -2.0 * inv * sy, -2.0 * inv * sz, inv, 1.0 + inv * (sx * sx + sy * sy + sz * sz)]
+    parts = [split3(v) for v in comps]
+    zero = jnp.zeros_like(r)
+    for group in range(3):
+        for part in range(3):
+            for comp in range(5):
+                value = parts[comp][group] if part + group < 3 else zero
+                rows[pl.ds(group * PARTS + part * 5 + comp, blocks, stride=3 * PARTS), :] = value
+        rows[pl.ds(group * PARTS + 15, blocks, stride=3 * PARTS), :] = zero
+    for b in range(blocks):
+        left[b] = rows[b * 3 * PARTS : (b + 1) * 3 * PARTS, :].T.astype(jnp.bfloat16)
+    for q, value in enumerate([yields[0], momentum[0], momentum[1], momentum[2], yields[1], zero, zero, zero]):
+        loads[pl.ds(q, blocks, stride=8), :] = value
+
+
+def one_block(b, table, count, feat, left, loads, moved):
+    listed = table.shape[0]
+    lhs = left[b]
+    norm_acc = jnp.zeros((128, 128), jnp.float32)
+    weights = []
+
+    def tile_of(j):
+        at = pl.multiple_of(table[j, b] * PARTS, PARTS)
+        return feat[pl.ds(at, PARTS), :].astype(jnp.bfloat16)
+
+    for j in range(0, listed, 2):
+        rhs = jnp.concatenate([tile_of(j), tile_of(j + 1)], axis=1)
+        u = jnp.dot(lhs, jnp.concatenate([rhs] * 3, axis=0), preferred_element_type=jnp.float32)
+        w = 1.0 / (u * u)
+        norm_acc = norm_acc + (w[:, :128] + w[:, 128:])
+        w1 = w.astype(jnp.bfloat16)
+        weights.append((w1, (w - w1.astype(jnp.float32)).astype(jnp.bfloat16)))
+    norm = jnp.sum(norm_acc.T, axis=0, keepdims=True)
+    lane = lax.broadcasted_iota(jnp.int32, (1, 128), 1)
+    live = jnp.where(b * 128 + lane < count[0], 1.0, 0.0)
+    coef = loads[pl.ds(pl.multiple_of(b * 8, 8), 8), :] * (live / norm)
+    c1 = coef.astype(jnp.bfloat16).astype(jnp.float32)
+    c2 = coef - c1
+    half = jnp.concatenate([c1, c2], axis=0).astype(jnp.bfloat16)
+    lhs2 = jnp.concatenate([half, half], axis=1)
+    for j in range(0, listed, 2):
+        got = jnp.dot(lhs2, jnp.concatenate(weights[j // 2], axis=0), preferred_element_type=jnp.float32)
+        both = got[0:8] + got[8:16]
+        start = pl.multiple_of((b * listed + j) * 8, 16)
+        moved[pl.ds(start, 8), :] = both[:, :128]
+        moved[pl.ds(start + 8, 8), :] = both[:, 128:]
+
+
+def scatter(sizes, table_rows, moved, out):
+    listed, blocks = table_rows.shape
+    slots, _, tiles, _ = out.shape
+    ids = table_rows[...]
+    slot, tile = ids // tiles, ids % tiles
+    nx, ny, nz = sizes
+    at = kind_of(slot // 9 - 1, nx) * kinds(ny) + kind_of(slot // 3 % 3 - 1, ny)
+    at = (at * kinds(nz) + kind_of(slot % 3 - 1, nz)) * tiles + tile
+    rows = slots * tiles
+    target = lax.broadcasted_iota(jnp.int32, (rows, listed), 0)
+    ones = []
+    for b in range(blocks):
+        ones.append(at[:, b : b + 1])
+    column = jnp.concatenate(ones, axis=0)
+    pairs = blocks * listed
+    hot = (column == lax.broadcasted_iota(jnp.int32, (pairs, rows), 1)).astype(jnp.float32)
+    hot = hot.T.astype(jnp.bfloat16)
+    hot = jnp.concatenate([hot, hot], axis=1)
+    for q in range(5):
+        value = moved[pl.ds(q, pairs, stride=8), :]
+        m1 = value.astype(jnp.bfloat16)
+        m2 = (value - m1.astype(jnp.float32)).astype(jnp.bfloat16)
+        got = jnp.dot(hot, jnp.concatenate([m1, m2], axis=0), preferred_element_type=jnp.float32)
+        for s in range(slots):
+            out[s, q] = got[s * tiles : (s + 1) * tiles]
+
+
+def deposit_kernel(sizes, unroll, table, count, table_rows, near, pos, radius, yields, momentum, out, feat, rows, left, loads, moved):
     blocks, listed = pos.shape[1], table.shape[0]
-    slots = near.shape[0]
-    nx, ny, nz = sizes
-    acc[...] = jnp.zeros_like(acc)
-    live_count = count[0]
-    lane = lax.broadcasted_iota(jnp.int32, (1, 128), 1)
-
-    def one_block(b):
-        row = pl.ds(b, 1)
-        r = radius[row, :]
-        inv = 1.0 / (r * r)
-        sx, sy, sz = (pos[k, row, :] - 0.5 for k in range(3))
-        left = rows_of(
-            [-2.0 * inv * sx, -2.0 * inv * sy, -2.0 * inv * sz, inv, 1.0 + inv * (sx * sx + sy * sy + sz * sz)]
-        )
-        a1, a2, a3 = split3(left)
-        lhs = jnp.concatenate([a1, a1, a2, a2, a1, a3], axis=0).T.astype(jnp.bfloat16)
-        norm_acc = jnp.zeros((128, 128), jnp.float32)
-        high, low, places = [], [], []
-        for j in range(listed):
-            tile_id = table[j, b]
-            slot, tile = tile_id // tiles_each, tile_id % tiles_each
-            a, bb, c = slot // 9 - 1, slot // 3 % 3 - 1, slot % 3 - 1
-            place = (kind_of(a, nx) * kinds(ny) + kind_of(bb, ny)) * kinds(nz) + kind_of(c, nz)
-            places.append(place * tiles_each + tile)
-            at = pl.ds(tile, 1)
-            gx = near[place, 0, at, :] + (a.astype(jnp.float32) - 0.5)
-            gy = near[place, 1, at, :] + (bb.astype(jnp.float32) - 0.5)
-            gz = near[place, 2, at, :] + (c.astype(jnp.float32) - 0.5)
-            mass = near[place, 3, at, :]
-            b1, b2, b3 = split3(rows_of([gx, gy, gz, gx * gx + gy * gy + gz * gz, jnp.ones_like(gx)]))
-            rhs = jnp.concatenate([b1, b2, b1, b2, b3, b1], axis=0).astype(jnp.bfloat16)
-            u = jnp.dot(lhs, rhs, preferred_element_type=jnp.float32)
-            w = 1.0 / (u * u)
-            norm_acc = norm_acc + w * mass
-            w1 = w.astype(jnp.bfloat16)
-            high.append(w1)
-            low.append((w - w1.astype(jnp.float32)).astype(jnp.bfloat16))
-        norm = jnp.sum(norm_acc.T, axis=0, keepdims=True)
-        live = jnp.where(b * 128 + lane < live_count, 1.0, 0.0)
-        scale = live / norm
-        loads = rows_of(
-            [yields[0, row, :], momentum[0, row, :], momentum[1, row, :], momentum[2, row, :], yields[1, row, :]]
-        )
-        c1, c2, c3 = split3(loads * scale)
-        coef = jnp.concatenate([c1, c2, c3, jnp.zeros_like(c1)], axis=0).astype(jnp.bfloat16)
-        for j in range(listed):
-            hi = jnp.dot(coef, high[j], preferred_element_type=jnp.float32)
-            lo = jnp.dot(coef[0:16], low[j], preferred_element_type=jnp.float32)
-            moved = hi[0:8] + (hi[8:16] + (hi[16:24] + (lo[0:8] + lo[8:16])))
-            start = pl.multiple_of(places[j] * 8, 8)
-            acc[pl.ds(start, 8), :] = acc[pl.ds(start, 8), :] + moved
+    slots, _, tiles, _ = near.shape
+    for slot, offset in enumerate(offsets()):
+        gas = [near[place_at(offset, sizes), k] for k in range(4)]
+        gas_features(gas, feat, slot, offset, tiles)
+    source_features(pos, radius, yields, momentum, rows, left, loads)
 
     def step(i, carry):
         for k in range(unroll):
-            one_block(i * unroll + k)
+            one_block(i * unroll + k, table, count, feat, left, loads, moved)
         return carry
 
-    used = jnp.minimum((live_count + 127) // 128, blocks)
-    lax.fori_loop(0, (used + unroll - 1) // unroll, step, 0)
-    for slot in range(slots):
-        for q in range(5):
-            out[slot, q] = acc[pl.ds(slot * tiles_each * 8 + q, tiles_each, stride=8), :]
+    lax.fori_loop(0, blocks // unroll, step, 0)
+    scatter(sizes, table_rows, moved, out)
 
 
 def local(sizes, gas_pos, gas_mass, source_pos, source_radius, source_yield, source_momentum, source_tiles, source_count):
@@ -267,18 +320,26 @@
         ],
         compiler_params=pltpu.CompilerParams(collective_id=0, has_side_effects=True, vmem_limit_bytes=LIMIT),
     )(gas_pos.reshape(3, tiles, 128), gas_mass.reshape(1, tiles, 128))
-    unroll = math.gcd(blocks, 4)
+    unroll = math.gcd(blocks, 2)
     smem = pl.BlockSpec(memory_space=pltpu.SMEM)
+    table = source_tiles.reshape(blocks, listed).T
     moved = pl.pallas_call(
-        functools.partial(deposit_kernel, sizes, tiles, unroll),
+        functools.partial(deposit_kernel, sizes, unroll),
         out_shape=pltpu.VMEM((slots, 5, tiles, 128), jnp.float32),
-        in_specs=[smem, smem] + [vmem] * 5,
+        in_specs=[smem, smem] + [vmem] * 6,
         out_specs=vmem,
-        scratch_shapes=[pltpu.VMEM((slots * tiles * 8, 128), jnp.float32)],
+        scratch_shapes=[
+            pltpu.VMEM((27 * tiles * PARTS, 128), jnp.float32),
+            pltpu.VMEM((blocks * 3 * PARTS, 128), jnp.float32),
+            pltpu.VMEM((blocks, 128, 3 * PARTS), jnp.bfloat16),
+            pltpu.VMEM((blocks * 8, 128), jnp.float32),
+            pltpu.VMEM((blocks * listed * 8, 128), jnp.float32),
+        ],
         compiler_params=pltpu.CompilerParams(vmem_limit_bytes=LIMIT),
     )(
-        source_tiles.reshape(blocks, listed).T,
+        table,
         source_count.reshape(1),
+        table,
         near,
         source_pos.reshape(3, blocks, 128),
         source_radius.reshape(blocks, 128),
@@ -290,7 +351,7 @@
     gain = pl.pallas_call(
         functools.partial(gather_kernel, sizes),
         out_shape=jax.ShapeDtypeStruct(piece, jnp.float32),
-        in_specs=[vmem],
+        in_specs=[vmem, vmem],
         out_specs=vmem,
         scratch_shapes=[
             pltpu.VMEM((sides, *piece), jnp.float32),
@@ -302,7 +363,7 @@
             pltpu.SemaphoreType.DMA((sides,)),
         ],
         compiler_params=pltpu.CompilerParams(collective_id=1, has_side_effects=True, vmem_limit_bytes=LIMIT),
-    )(moved)
+    )(moved, gas_mass.reshape(1, tiles, 128))
     return gain.reshape(5, 1, 1, 1, gas_size)
 
 

time: 38.1 us -> 38.2 us (level)
  Pallas kernels: 34.7 us -> 35.1 us
    pallas_call x1, Pallas kernels: 7.52 us -> 9.07 us  [local(): pl.pallas_call(functools.partial(deposit_kernel, sizes, unroll), out_shap...]
    pallas_call x1, Pallas kernels: 13.4 us -> 12.3 us  [local(): pl.pallas_call(functools.partial(gather_kernel, sizes), out_shape=jax.Sha...]
where the time goes in v1:
time: 38.2 us; the launch traced here: 38 us
  Pallas kernels  35.1 us (92%)
  local copies, waits for them, and re-layouts  2.07 us (5%)
  between operations  0.74 us (2%)
    pallas_call x1, Pallas kernels, local(): pl.pallas_call(functools.partial(spread_kernel, sizes), out_shape=pltpu.V...  13.8 us
    pallas_call x1, Pallas kernels, local(): pl.pallas_call(functools.partial(gather_kernel, sizes), out_shape=jax.Sha...  12.3 us
    pallas_call x1, Pallas kernels, local(): pl.pallas_call(functools.partial(deposit_kernel, sizes, unroll), out_shap...  9.07 us
    unnamed x15, local copies, waits for them, and re-layouts  2.07 us

profile of v1, /device:TPU:0, one launch (start us, length us, event | category | flops | bytes accessed | tf_op | source)
XLA Modules:
  0.0 38.0 jit_solution(11443550129212032741)
XLA Ops:
  0.7 0.0 copy-start
  0.7 0.7 %copy-done = f32[1,1,1,2048]{3,2,1,0:T(1,128)S(1)} copy-done((f32[1,1,1,2048]{3,2,1,0:T(1,128)S(1)}, f32[1,1,1,2048]{3,2,1,0:T(1,128)}, u32[]{:S(2)}) %copy-start) | copy-done | bytes 8216
  1.4 0.0 copy-start.1
  1.4 0.7 %copy-done.1 = f32[3,1,1,1,2048]{4,3,2,1,0:T(1,128)S(1)} copy-done((f32[3,1,1,1,2048]{4,3,2,1,0:T(1,128)S(1)}, f32[3,1,1,1,2048]{4,3,2,1,0:T(1,128)}, u32[]{:S(2)}) %copy-start.1) | copy-done | bytes 24600
  2.1 0.0 copy-start.2
  2.1 0.0 copy-start.3
  2.1 0.0 copy-start.4
  2.1 0.0 copy-start.5
  2.1 0.0 copy-start.6
  2.1 13.8 %shard_map.82.near = f32[18,4,16,128]{3,2,1,0:T(8,128)S(1)} custom-call(f32[3,16,128]{2,1,0:T(8,128)S(1)} %bitcast.15, f32[1,16,128]{2,1,0:T(8,128)S(1)} %bitcast.13), custom_call_target="tpu_custom_call" | custom-call | tf_op jit(solution)/shard_map/pallas_call | solution.py:311
  15.9 0.0 copy-done.2
  15.9 0.0 copy-done.3
  15.9 0.0 copy-done.4
  15.9 0.0 copy-done.5
  15.9 0.0 copy-done.6
  15.9 9.1 %shard_map.83.moved = f32[18,5,16,128]{3,2,1,0:T(8,128)S(1)} custom-call(s32[8,16]{1,0:T(8,128)S(1)} %bitcast.19, s32[1]{0:T(128)} %bitcast.11.count, s32[8,16]{1,0:T(8,128)S(1)} %bitcast.20, f32[18,4,16,128]{3,2,1,0:T(8,128)S(1)} %shard_map.82.near, f32[3,16,128]{2,1,0:T(8,128)S(1)} %bitcast.16, f32[16,128]{1,0:T(8,128)S(1)} %bitcast.21, ...), custom_call_target="tpu_custom_call" | custom-call | tf_op jit(solution)/shard_map/pallas_call | solution.py:326
  25.0 12.3 %shard_map.84 = f32[5,16,128]{2,1,0:T(8,128)S(1)} custom-call(f32[18,5,16,128]{3,2,1,0:T(8,128)S(1)} %shard_map.83.moved, f32[1,16,128]{2,1,0:T(8,128)S(1)} %bitcast.14), custom_call_target="tpu_custom_call" | custom-call | tf_op jit(solution)/shard_map/pallas_call | solution.py:351
  37.3 0.6 %copy.13 = f32[5,1,1,1,2048]{4,3,2,1,0:T(1,128)} copy(f32[5,1,1,1,2048]{4,3,2,1,0:T(1,128)S(1)} %bitcast.12) | data formatting | bytes 81920
Async XLA Ops:
  0.7 0.7 %copy-start = (f32[1,1,1,2048]{3,2,1,0:T(1,128)S(1)}, f32[1,1,1,2048]{3,2,1,0:T(1,128)}, u32[]{:S(2)}) copy-start(f32[1,1,1,2048]{3,2,1,0:T(1,128)} %param.9) | copy-start | bytes 24580
  1.4 0.7 %copy-start.1 = (f32[3,1,1,1,2048]{4,3,2,1,0:T(1,128)S(1)}, f32[3,1,1,1,2048]{4,3,2,1,0:T(1,128)}, u32[]{:S(2)}) copy-start(f32[3,1,1,1,2048]{4,3,2,1,0:T(1,128)} %param.8) | copy-start | bytes 73732
  2.1 13.8 %copy-start.2 = (f32[3,1,1,1,2048]{4,3,2,1,0:T(1,128)S(1)}, f32[3,1,1,1,2048]{4,3,2,1,0:T(1,128)}, u32[]{:S(2)}) copy-start(f32[3,1,1,1,2048]{4,3,2,1,0:T(1,128)} %param.10) | copy-start | bytes 73732
  2.1 13.8 %copy-start.3 = (f32[3,1,1,1,2048]{4,3,2,1,0:T(1,128)S(1)}, f32[3,1,1,1,2048]{4,3,2,1,0:T(1,128)}, u32[]{:S(2)}) copy-start(f32[3,1,1,1,2048]{4,3,2,1,0:T(1,128)} %param.13) | copy-start | bytes 73732
  2.1 13.8 %copy-start.4 = (f32[2,1,1,1,2048]{4,3,2,1,0:T(1,128)S(1)}, f32[2,1,1,1,2048]{4,3,2,1,0:T(1,128)}, u32[]{:S(2)}) copy-start(f32[2,1,1,1,2048]{4,3,2,1,0:T(1,128)} %param.12) | copy-start | bytes 49156
  2.1 13.8 %copy-start.5 = (s32[1,1,1,16,8]{3,4,2,1,0:T(8,128)S(1)}, s32[1,1,1,16,8]{3,4,2,1,0:T(8,128)}, u32[]{:S(2)}) copy-start(s32[1,1,1,16,8]{3,4,2,1,0:T(8,128)} %param.14) | copy-start | bytes 1540
  2.1 13.8 %copy-start.6 = (f32[1,1,1,2048]{3,2,1,0:T(1,128)S(1)}, f32[1,1,1,2048]{3,2,1,0:T(1,128)}, u32[]{:S(2)}) copy-start(f32[1,1,1,2048]{3,2,1,0:T(1,128)} %param.11) | copy-start | bytes 24580

commit v2 on v0

v2 whole, which is shorter than its diff:
```python
import functools
import math

import jax
import jax.numpy as jnp
from jax import lax
from jax.experimental import pallas as pl
from jax.experimental.pallas import tpu as pltpu
from jax.sharding import PartitionSpec as P


def kinds(count):
    return min(count, 3)


def kind_of(offset, count):
    if count >= 3:
        return offset + 1
    if count == 2:
        return jnp.abs(offset)
    return offset * 0


def own_kind(count):
    return 1 if count >= 3 else 0


def steps_of(count):
    if count >= 3:
        return ((0, -1), (2, 1))
    return ((1, 1),) if count == 2 else ()


MESH = pl.DeviceIdType.MESH
LIMIT = 48 * 1024 * 1024


def shifted(axis, count, step):
    return lax.rem(lax.axis_index(axis) + step + count, count)


def columns_of(sizes):
    nx, ny, _ = sizes
    choices_x = steps_of(nx) + ((own_kind(nx), 0),)
    choices_y = ((own_kind(ny), 0),) + steps_of(ny)
    return [
        ((i, j), {"gx": shifted("gx", nx, dx), "gy": shifted("gy", ny, dy)})
        for i, dx in choices_x
        for j, dy in choices_y
        if dx or dy
    ]


def cores_of(sizes):
    return [(k, {"gz": shifted("gz", sizes[2], dz)}) for k, dz in steps_of(sizes[2])]


def greet(sizes):
    barrier = pltpu.get_barrier_semaphore()
    peers = columns_of(sizes) + cores_of(sizes)
    for _, device in peers:
        pl.semaphore_signal(barrier, inc=1, device_id=device, device_id_type=MESH)
    if peers:
        pl.semaphore_wait(barrier, len(peers))


def facing(kind, count):
    return 2 - kind if count >= 3 else kind


PARTS = 16


def split3(value):
    first = value.astype(jnp.bfloat16).astype(jnp.float32)
    rest = value - first
    second = rest.astype(jnp.bfloat16).astype(jnp.float32)
    return first, second, rest - second


def offsets():
    return [(a, b, c) for a in (-1, 0, 1) for b in (-1, 0, 1) for c in (-1, 0, 1)]


def kind_at(offset, count):
    if count >= 3:
        return offset + 1
    return abs(offset) if count == 2 else 0


def place_at(offset, sizes):
    i, j, k = (kind_at(o, n) for o, n in zip(offset, sizes))
    return (i * kinds(sizes[1]) + j) * kinds(sizes[2]) + k


def role_places(role, sizes):
    places = [place_at(o, sizes) for o in offsets() if (o[0] != 0, o[1] != 0) == (role >= 2, role % 2 == 1)]
    return sorted(set(places))


def role_slots(role):
    return [n for n, o in enumerate(offsets()) if (o[0] != 0, o[1] != 0) == (role >= 2, role % 2 == 1)]


def gas_features(gas, feat, slot, offset):
    tiles = gas[3].shape[0]
    px, py, pz = (gas[k] + (offset[k] - 0.5) for k in range(3))
    root = lax.rsqrt(gas[3])
    square = (px * px + py * py + pz * pz) * root
    base = [n for role in range(4) for n in role_slots(role)].index(slot) * tiles
    for comp, value in enumerate((px * root, py * root, pz * root, square, root)):
        for part, piece in enumerate(split3(value)):
            at = (part * 5 + comp) * 128
            feat[base : base + tiles, at : at + 128] = piece.astype(jnp.bfloat16)


def source_features(pos, radius, rows, left):
    blocks = pos.shape[1]
    r = radius[...]
    inv = 1.0 / (r * r)
    sx, sy, sz = (pos[k] - 0.5 for k in range(3))
    comps = [-2.0 * inv * sx, -2.0 * inv * sy, -2.0 * inv * sz, inv, 1.0 + inv * (sx * sx + sy * sy + sz * sz)]
    parts = [split3(v) for v in comps]
    zero = jnp.zeros_like(r)
    for group in range(3):
        for part in range(3):
            for comp in range(5):
                value = parts[comp][group] if part + group < 3 else zero
                rows[pl.ds(group * PARTS + part * 5 + comp, blocks, stride=3 * PARTS), :] = value
        rows[pl.ds(group * PARTS + 15, blocks, stride=3 * PARTS), :] = zero
    for b in range(blocks):
        left[b] = rows[b * 3 * PARTS : (b + 1) * 3 * PARTS, :].T.astype(jnp.bfloat16)


def over_blocks(blocks, unroll, body):
    def step(i, carry):
        for k in range(unroll):
            body(i * unroll + k)
        return carry

    lax.fori_loop(0, blocks // unroll, step, 0)


def gather(role, tiles, feat, hot_in, picked):
    slots = [n for r in range(4) for n in role_slots(r)]
    first = slots.index(role_slots(role)[0]) * tiles
    depth = len(role_slots(role)) * tiles
    pairs = hot_in.shape[1]
    got = jnp.dot(hot_in[role, :, 0:depth], feat[first : first + depth, :], preferred_element_type=jnp.float32)
    for row in range(PARTS - 1):
        picked[role % 2, pl.ds(row, pairs, stride=PARTS), :] = got[:, row * 128 : row * 128 + 128]


def weigh(role, picked, left, weights, sums, norms, unroll):
    blocks = left.shape[0]

    def body(b):
        near = []
        for z in range(2):
            at = pl.multiple_of((z * blocks + b) * PARTS, PARTS)
            near.append(picked[role % 2, pl.ds(at, PARTS), :].astype(jnp.bfloat16))
        rhs = jnp.concatenate([jnp.concatenate(near, axis=1)] * 3, axis=0)
        u = jnp.dot(left[b], rhs, preferred_element_type=jnp.float32)
        w = 1.0 / (u * u)
        part = w[:, :128] + w[:, 128:]
        if role:
            part = sums[b] + part
        if role < 3:
            sums[b] = part
        else:
            norms[pl.ds(b, 1), :] = jnp.sum(part.T, axis=0, keepdims=True)
        w1 = w.astype(jnp.bfloat16)
        weights[role, b, 0:128] = w1
        weights[role, b, 128:256] = (w - w1.astype(jnp.float32)).astype(jnp.bfloat16)

    over_blocks(blocks, unroll, body)


def normalise(count, norms, yields, momentum, loads):
    blocks = norms.shape[0]
    lane = lax.broadcasted_iota(jnp.int32, (blocks, 128), 1)
    index = lax.broadcasted_iota(jnp.int32, (blocks, 128), 0) * 128 + lane
    scale = jnp.where(index < count[0], 1.0, 0.0) / norms[...]
    zero = jnp.zeros_like(scale)
    for q, value in enumerate([yields[0], momentum[0], momentum[1], momentum[2], yields[1], zero, zero, zero]):
        coef = value * scale
        high = coef.astype(jnp.bfloat16).astype(jnp.float32)
        loads[pl.ds(q, blocks, stride=16), :] = high
        loads[pl.ds(q + 8, blocks, stride=16), :] = coef - high


def deposit(role, loads, weights, moved, unroll):
    blocks = weights.shape[1]

    def body(b):
        half = loads[pl.ds(pl.multiple_of(b * 16, 16), 16), :].astype(jnp.bfloat16)
        got = jnp.dot(jnp.concatenate([half, half], axis=1), weights[role, b], preferred_element_type=jnp.float32)
        both = got[0:8] + got[8:16]
        for z in range(2):
            start = pl.multiple_of((z * blocks + b) * 8, 8)
            moved[role, pl.ds(start, 8), :] = both[:, z * 128 : z * 128 + 128]

    over_blocks(blocks, unroll, body)


def one_hots(sizes, tiles, table_rows, hot_in, hot_out):
    nx, ny, nz = sizes
    ids = table_rows[...]
    slot, tile = ids // tiles, ids % tiles
    at = kind_of(slot // 9 - 1, nx) * kinds(ny) + kind_of(slot // 3 % 3 - 1, ny)
    at = (at * kinds(nz) + kind_of(slot % 3 - 1, nz)) * tiles + tile
    flip_a = slot[0:1] // 9 == 0
    flip_b = slot[0:1] // 3 % 3 == 0

    def pick(values, role):
        row = []
        for z in range(2):
            low, high = (
                jnp.where(flip_b, values[4 * a + z + 2 : 4 * a + z + 3], values[4 * a + z : 4 * a + z + 1])
                if role % 2 == 0
                else jnp.where(flip_b, values[4 * a + z : 4 * a + z + 1], values[4 * a + z + 2 : 4 * a + z + 3])
                for a in range(2)
            )
            row.append(jnp.where(flip_a, high, low) if role < 2 else jnp.where(flip_a, low, high))
        return jnp.concatenate(row, axis=1)

    for role in range(4):
        source, target = pick(ids, role), pick(at, role)
        pairs = source.shape[1]
        index = lax.broadcasted_iota(jnp.int32, (tiles, pairs), 0)
        hot = [(index + n * tiles == source).astype(jnp.float32) for n in role_slots(role)]
        depth = len(hot) * tiles
        hot_in[role, :, 0:depth] = jnp.concatenate(hot, axis=0).T.astype(jnp.bfloat16)
        hot = [(index + n * tiles == target).astype(jnp.float32) for n in role_places(role, sizes)]
        hot = jnp.concatenate(hot, axis=0).astype(jnp.bfloat16)
        hot_out[role, 0 : hot.shape[0], :] = jnp.concatenate([hot, hot], axis=1)


def scatter(role, sizes, hot_out, moved, out, done):
    tiles = out.shape[2]
    places = role_places(role, sizes)
    pairs = hot_out.shape[2] // 2
    values = jnp.concatenate([moved[role, pl.ds(q, pairs, stride=8), :] for q in range(5)], axis=1)
    m1 = values.astype(jnp.bfloat16)
    m2 = (values - m1.astype(jnp.float32)).astype(jnp.bfloat16)
    hot = hot_out[role, 0 : len(places) * tiles, :]
    got = jnp.dot(hot, jnp.concatenate([m1, m2], axis=0), preferred_element_type=jnp.float32)
    for n, place in enumerate(places):
        for q in range(5):
            value = got[n * tiles : (n + 1) * tiles, q * 128 : (q + 1) * 128]
            out[place, q] = out[place, q] + value if place in done else value
        done.add(place)


def core_scratch(blocks, tiles):
    return [
        pltpu.VMEM((27 * tiles, (PARTS - 1) * 128), jnp.bfloat16),
        pltpu.VMEM((blocks * 3 * PARTS, 128), jnp.float32),
        pltpu.VMEM((blocks, 128, 3 * PARTS), jnp.bfloat16),
        pltpu.VMEM((4, blocks, 256, 256), jnp.bfloat16),
        pltpu.VMEM((blocks, 128, 128), jnp.float32),
        pltpu.VMEM((blocks, 128), jnp.float32),
        pltpu.VMEM((blocks * 16, 128), jnp.float32),
        pltpu.VMEM((4, blocks * 16, 128), jnp.float32),
        pltpu.VMEM((4, 2 * blocks, 12 * tiles), jnp.bfloat16),
        pltpu.VMEM((4, 12 * tiles, 4 * blocks), jnp.bfloat16),
        pltpu.VMEM((2, 2 * blocks * PARTS, 128), jnp.float32),
    ]


def fused_kernel(sizes, pos, mass, table, count, spos, sradius, syield, smomentum, out, *scratch):
    (near, count_s, table_v, pos_v, radius_v, yield_v, momentum_v, deposits, part, got_z, got) = scratch[:11]
    (feat, rows, left, weights, sums, norms, loads, moved, hot_in, hot_out, picked) = scratch[11:22]
    local_sem, send_sem, recv_sem, gsend_z, grecv_z, gsend, grecv = scratch[22:]
    nx, ny, nz = sizes
    own = tuple(own_kind(n) for n in sizes)
    tiles = near.shape[2]
    blocks = pos_v.shape[1]
    unroll = math.gcd(blocks, 16)

    def place(i, j, k):
        return (i * kinds(ny) + j) * kinds(nz) + k

    home = place(*own)
    gas_in = [
        pltpu.make_async_copy(pos, near.at[home, pl.ds(0, 3)], local_sem.at[0]),
        pltpu.make_async_copy(mass, near.at[home, pl.ds(3, 1)], local_sem.at[1]),
    ]
    pairs = [(spos, pos_v), (sradius, radius_v), (syield, yield_v), (smomentum, momentum_v)]
    pairs += [(count, count_s), (table, table_v)]
    rest_in = [pltpu.make_async_copy(src, dst, local_sem.at[2 + n]) for n, (src, dst) in enumerate(pairs)]
    for copy in gas_in + rest_in:
        copy.start()
    greet(sizes)
    for copy in gas_in:
        copy.wait()
    copies = {}
    finished = []

    def send(slot, there, device):
        target = place(*there)
        copy = pltpu.make_async_remote_copy(
            src_ref=near.at[place(*slot)],
            dst_ref=near.at[target],
            send_sem=send_sem.at[target],
            recv_sem=recv_sem.at[target],
            device_id=device,
            device_id_type=MESH,
        )
        copy.start()
        copies[there] = copy
        finished.append(copy)

    def to_cores(i, j):
        for k, device in cores_of(sizes):
            send((i, j, own[2]), (i, j, facing(k, nz)), device)

    columns = columns_of(sizes)
    for (i, j), device in columns:
        send(own, (facing(i, nx), facing(j, ny), own[2]), device)
    to_cores(own[0], own[1])
    for copy in rest_in:
        copy.wait()

    def features(i, j, k):
        for slot, offset in enumerate(offsets()):
            if place_at(offset, sizes) == place(i, j, k):
                gas_features([near[place(i, j, k), c] for c in range(4)], feat, slot, offset)

    def weigh_role(role):
        gather(role, tiles, feat, hot_in, picked)
        weigh(role, picked, left, weights, sums, norms, unroll)

    source_features(pos_v, radius_v, rows, left)
    one_hots(sizes, tiles, table_v, hot_in, hot_out)
    spare = jnp.zeros((2 * blocks, 128), jnp.float32)
    for side in range(2):
        picked[side, pl.ds(PARTS - 1, 2 * blocks, stride=PARTS), :] = spare
    features(*own)
    for k, _ in steps_of(nz):
        copies[own[0], own[1], k].wait_recv()
        features(own[0], own[1], k)
    weigh_role(0)
    across = [at for at, _ in columns if at[0] != own[0]]
    along = [at for at, _ in columns if at[0] == own[0]]
    for at in along + across:
        copies[at[0], at[1], own[2]].wait_recv()
        to_cores(*at)
        features(at[0], at[1], own[2])
    for role in (1, 2, 3):
        for i, j in along + across:
            if (i != own[0], j != own[1]) == (role >= 2, role % 2 == 1):
                for k, _ in steps_of(nz):
                    copies[i, j, k].wait_recv()
                    features(i, j, k)
        weigh_role(role)
    normalise(count_s, norms, yield_v, momentum_v, loads)
    done = set()
    along_z, arriving = {}, {}

    def send_gain(src, dst, send_at, recv_at, device):
        copy = pltpu.make_async_remote_copy(
            src_ref=src, dst_ref=dst, send_sem=send_at, recv_sem=recv_at, device_id=device, device_id_type=MESH
        )
        copy.start()
        finished.append(copy)
        return copy

    def role_of(at):
        return 2 * (at[0] != own[0]) + (at[1] != own[1])

    def send_z(i, j):
        for k, device in cores_of(sizes):
            at = place(i, j, k)
            along_z[i, j, k] = send_gain(deposits.at[at], got_z.at[at], gsend_z.at[at], grecv_z.at[at], device)

    for role in (3, 2, 1, 0):
        deposit(role, loads, weights, moved, unroll)
        scatter(role, sizes, hot_out, moved, deposits, done)
        for i, j in [at for at, _ in columns] + [own[:2]]:
            if role_of((i, j)) == role:
                send_z(i, j)
    ordered = sorted(columns, key=lambda c: -role_of(c[0]))

    def send_part(index):
        (i, j), device = ordered[index]
        at = i * kinds(ny) + j
        arriving[at] = send_gain(part.at[at], got.at[at], gsend.at[at], grecv.at[at], device)

    order = [at for at, _ in ordered] + [own[:2]]
    for index, (i, j) in enumerate(order):
        total = deposits[place(i, j, own[2])]
        for k, _ in steps_of(nz):
            along_z[i, j, k].wait_recv()
            total = total + got_z[place(i, j, k)]
        if index < len(ordered):
            part[i * kinds(ny) + j] = total
        if index:
            send_part(index - 1)
    for at in reversed(list(arriving)):
        arriving[at].wait_recv()
        total = total + got[at]
    out[...] = total / near[home, 3]
    for copy in finished:
        copy.wait_send()


def local(sizes, gas_pos, gas_mass, source_pos, source_radius, source_yield, source_momentum, source_tiles, source_count):
    gas_size = gas_pos.shape[-1]
    tiles = gas_size // 128
    blocks = source_pos.shape[-1] // 128
    listed = source_tiles.shape[-1]
    slots = kinds(sizes[0]) * kinds(sizes[1]) * kinds(sizes[2])
    sides = kinds(sizes[0]) * kinds(sizes[1])
    piece = (5, tiles, 128)
    given = pl.BlockSpec(memory_space=pl.ANY)
    dma = pltpu.SemaphoreType.DMA
    gain = pl.pallas_call(
        functools.partial(fused_kernel, sizes),
        out_shape=jax.ShapeDtypeStruct(piece, jnp.float32),
        in_specs=[given] * 8,
        out_specs=pl.BlockSpec(memory_space=pltpu.VMEM),
        scratch_shapes=[
            pltpu.VMEM((slots, 4, tiles, 128), jnp.float32),
            pltpu.SMEM((1,), jnp.int32),
            pltpu.VMEM((listed, blocks), jnp.int32),
            pltpu.VMEM((3, blocks, 128), jnp.float32),
            pltpu.VMEM((blocks, 128), jnp.float32),
            pltpu.VMEM((2, blocks, 128), jnp.float32),
            pltpu.VMEM((3, blocks, 128), jnp.float32),
            pltpu.VMEM((slots, *piece), jnp.float32),
            pltpu.VMEM((sides, *piece), jnp.float32),
            pltpu.VMEM((slots, *piece), jnp.float32),
            pltpu.VMEM((sides, *piece), jnp.float32),
            *core_scratch(blocks, tiles),
            dma((8,)),
            dma((slots,)),
            dma((slots,)),
            dma((slots,)),
            dma((slots,)),
            dma((sides,)),
            dma((sides,)),
        ],
        compiler_params=pltpu.CompilerParams(collective_id=0, has_side_effects=True, vmem_limit_bytes=LIMIT),
    )(
        gas_pos.reshape(3, tiles, 128),
        gas_mass.reshape(1, tiles, 128),
        source_tiles.reshape(blocks, listed).T,
        source_count.reshape(1),
        source_pos.reshape(3, blocks, 128),
        source_radius.reshape(blocks, 128),
        source_yield.reshape(2, blocks, 128),
        source_momentum.reshape(3, blocks, 128),
    )
    return gain.reshape(5, 1, 1, 1, gas_size)


def solution(mesh):
    sizes = (mesh.shape["gx"], mesh.shape["gy"], mesh.shape["gz"])
    in_specs = (
        P(None, "gx", "gy", "gz", None),
        P("gx", "gy", "gz", None),
        P(None, "gx", "gy", "gz", None),
        P("gx", "gy", "gz", None),
        P(None, "gx", "gy", "gz", None),
        P(None, "gx", "gy", "gz", None),
        P("gx", "gy", "gz", None, None),
        P("gx", "gy", "gz"),
    )
    out_specs = P(None, "gx", "gy", "gz", None)
    return jax.shard_map(
        functools.partial(local, sizes), mesh=mesh, in_specs=in_specs, out_specs=out_specs, check_vma=False
    )
```

time: 38.1 us -> 34.1 us (0.90)
  Pallas kernels: 34.7 us -> 27.9 us
  local copies, waits for them, and re-layouts: 2.07 us -> 4.98 us
    pallas_call x3 -> x1, Pallas kernels: 34.7 us -> 27.9 us  [local(): pl.pallas_call(functools.partial(fused_kernel, sizes), out_shape=jax.Shap...]
    unnamed x15, local copies, waits for them, and re-layouts: 2.07 us -> 4.98 us
where the time goes in v2:
time: 34.1 us; the launch traced here: 33.6 us
  Pallas kernels  27.9 us (82%)
  local copies, waits for them, and re-layouts  4.98 us (15%)
  between operations  0.68 us (2%)
    pallas_call x1, Pallas kernels, local(): pl.pallas_call(functools.partial(fused_kernel, sizes), out_shape=jax.Shap...  27.9 us
    unnamed x15, local copies, waits for them, and re-layouts  4.98 us

profile of v2, /device:TPU:0, one launch (start us, length us, event | category | flops | bytes accessed | tf_op | source)
XLA Modules:
  0.0 33.6 jit_solution(15704050124345442203)
XLA Ops:
  0.0 0.0 copy-start.3
  0.7 0.1 copy-done.3
  0.7 0.0 copy-start
  0.7 0.7 %copy-done = f32[3,1,1,1,2048]{4,3,2,1,0:T(1,128)S(1)} copy-done((f32[3,1,1,1,2048]{4,3,2,1,0:T(1,128)S(1)}, f32[3,1,1,1,2048]{4,3,2,1,0:T(1,128)}, u32[]{:S(2)}) %copy-start) | copy-done | bytes 24600
  1.5 0.0 copy-start.1
  1.5 0.7 %copy-done.1 = f32[3,1,1,1,2048]{4,3,2,1,0:T(1,128)S(1)} copy-done((f32[3,1,1,1,2048]{4,3,2,1,0:T(1,128)S(1)}, f32[3,1,1,1,2048]{4,3,2,1,0:T(1,128)}, u32[]{:S(2)}) %copy-start.1) | copy-done | bytes 24600
  2.2 0.0 copy-start.2
  2.2 0.7 %copy-done.2 = f32[3,1,1,1,2048]{4,3,2,1,0:T(1,128)S(1)} copy-done((f32[3,1,1,1,2048]{4,3,2,1,0:T(1,128)S(1)}, f32[3,1,1,1,2048]{4,3,2,1,0:T(1,128)}, u32[]{:S(2)}) %copy-start.2) | copy-done | bytes 24600
  2.9 0.0 copy-start.4
  3.0 0.7 %copy-done.4 = f32[1,1,1,2048]{3,2,1,0:T(1,128)S(1)} copy-done((f32[1,1,1,2048]{3,2,1,0:T(1,128)S(1)}, f32[1,1,1,2048]{3,2,1,0:T(1,128)}, u32[]{:S(2)}) %copy-start.4) | copy-done | bytes 8216
  3.6 0.0 copy-start.5
  3.6 0.7 %copy-done.5 = f32[1,1,1,2048]{3,2,1,0:T(1,128)S(1)} copy-done((f32[1,1,1,2048]{3,2,1,0:T(1,128)S(1)}, f32[1,1,1,2048]{3,2,1,0:T(1,128)}, u32[]{:S(2)}) %copy-start.5) | copy-done | bytes 8216
  4.3 0.0 copy-start.6
  4.3 0.7 %copy-done.6 = s32[1,1,1,16,8]{3,4,2,1,0:T(8,128)S(1)} copy-done((s32[1,1,1,16,8]{3,4,2,1,0:T(8,128)S(1)}, s32[1,1,1,16,8]{3,4,2,1,0:T(8,128)}, u32[]{:S(2)}) %copy-start.6) | copy-done | bytes 536
  5.0 27.9 %shard_map.82 = f32[5,16,128]{2,1,0:T(8,128)S(1)} custom-call(f32[3,16,128]{2,1,0:T(8,128)S(1)} %bitcast.13, f32[1,16,128]{2,1,0:T(8,128)S(1)} %bitcast.17, s32[8,16]{1,0:T(8,128)S(1)} %bitcast.19, s32[1]{0:T(128)} %bitcast.11.count, f32[3,16,128]{2,1,0:T(8,128)S(1)} %bitcast.14, f32[16,128]{1,0:T(8,128)S(1)} %bitcast.18, f32[2,16,128]{2,1,0:T(8,128)S(1)} %bitcast.16, ...), custom_call_target="tpu_custom_call" | custom-call | tf_op jit(solution)/shard_map/pallas_call | solution.py:418
  33.0 0.6 %copy.13 = f32[5,1,1,1,2048]{4,3,2,1,0:T(1,128)} copy(f32[5,1,1,1,2048]{4,3,2,1,0:T(1,128)S(1)} %bitcast.12) | data formatting | bytes 81920
Async XLA Ops:
  0.0 0.7 %copy-start.3 = (f32[2,1,1,1,2048]{4,3,2,1,0:T(1,128)S(1)}, f32[2,1,1,1,2048]{4,3,2,1,0:T(1,128)}, u32[]{:S(2)}) copy-start(f32[2,1,1,1,2048]{4,3,2,1,0:T(1,128)} %param.12) | copy-start | bytes 49156
  0.7 0.7 %copy-start = (f32[3,1,1,1,2048]{4,3,2,1,0:T(1,128)S(1)}, f32[3,1,1,1,2048]{4,3,2,1,0:T(1,128)}, u32[]{:S(2)}) copy-start(f32[3,1,1,1,2048]{4,3,2,1,0:T(1,128)} %param.8) | copy-start | bytes 73732
  1.5 0.7 %copy-start.1 = (f32[3,1,1,1,2048]{4,3,2,1,0:T(1,128)S(1)}, f32[3,1,1,1,2048]{4,3,2,1,0:T(1,128)}, u32[]{:S(2)}) copy-start(f32[3,1,1,1,2048]{4,3,2,1,0:T(1,128)} %param.10) | copy-start | bytes 73732
  2.2 0.7 %copy-start.2 = (f32[3,1,1,1,2048]{4,3,2,1,0:T(1,128)S(1)}, f32[3,1,1,1,2048]{4,3,2,1,0:T(1,128)}, u32[]{:S(2)}) copy-start(f32[3,1,1,1,2048]{4,3,2,1,0:T(1,128)} %param.13) | copy-start | bytes 73732
  2.9 0.7 %copy-start.4 = (f32[1,1,1,2048]{3,2,1,0:T(1,128)S(1)}, f32[1,1,1,2048]{3,2,1,0:T(1,128)}, u32[]{:S(2)}) copy-start(f32[1,1,1,2048]{3,2,1,0:T(1,128)} %param.9) | copy-start | bytes 24580
  3.6 0.7 %copy-start.5 = (f32[1,1,1,2048]{3,2,1,0:T(1,128)S(1)}, f32[1,1,1,2048]{3,2,1,0:T(1,128)}, u32[]{:S(2)}) copy-start(f32[1,1,1,2048]{3,2,1,0:T(1,128)} %param.11) | copy-start | bytes 24580
  4.3 0.7 %copy-start.6 = (s32[1,1,1,16,8]{3,4,2,1,0:T(8,128)S(1)}, s32[1,1,1,16,8]{3,4,2,1,0:T(8,128)}, u32[]{:S(2)}) copy-start(s32[1,1,1,16,8]{3,4,2,1,0:T(8,128)} %param.14) | copy-start | bytes 1540

commit v3 on v2

--- a/solution.py
+++ b/solution.py
@@ -32,7 +32,7 @@
 
 
 MESH = pl.DeviceIdType.MESH
-LIMIT = 48 * 1024 * 1024
+LIMIT = 67_043_328 - 64 * 1024
 
 
 def shifted(axis, count, step):
@@ -180,7 +180,7 @@
     blocks = norms.shape[0]
     lane = lax.broadcasted_iota(jnp.int32, (blocks, 128), 1)
     index = lax.broadcasted_iota(jnp.int32, (blocks, 128), 0) * 128 + lane
-    scale = jnp.where(index < count[0], 1.0, 0.0) / norms[...]
+    scale = jnp.where(index < count[0, 0], 1.0, 0.0) / norms[...]
     zero = jnp.zeros_like(scale)
     for q, value in enumerate([yields[0], momentum[0], momentum[1], momentum[2], yields[1], zero, zero, zero]):
         coef = value * scale
@@ -413,16 +413,16 @@
     slots = kinds(sizes[0]) * kinds(sizes[1]) * kinds(sizes[2])
     sides = kinds(sizes[0]) * kinds(sizes[1])
     piece = (5, tiles, 128)
-    given = pl.BlockSpec(memory_space=pl.ANY)
+    given = pl.BlockSpec(memory_space=pltpu.HBM)
     dma = pltpu.SemaphoreType.DMA
     gain = pl.pallas_call(
         functools.partial(fused_kernel, sizes),
-        out_shape=jax.ShapeDtypeStruct(piece, jnp.float32),
+        out_shape=pltpu.VMEM(piece, jnp.float32),
         in_specs=[given] * 8,
         out_specs=pl.BlockSpec(memory_space=pltpu.VMEM),
         scratch_shapes=[
             pltpu.VMEM((slots, 4, tiles, 128), jnp.float32),
-            pltpu.SMEM((1,), jnp.int32),
+            pltpu.SMEM((1, 1), jnp.int32),
             pltpu.VMEM((listed, blocks), jnp.int32),
             pltpu.VMEM((3, blocks, 128), jnp.float32),
             pltpu.VMEM((blocks, 128), jnp.float32),
@@ -446,7 +446,7 @@
         gas_pos.reshape(3, tiles, 128),
         gas_mass.reshape(1, tiles, 128),
         source_tiles.reshape(blocks, listed).T,
-        source_count.reshape(1),
+        source_count.reshape(1, 1),
         source_pos.reshape(3, blocks, 128),
         source_radius.reshape(blocks, 128),
         source_yield.reshape(2, blocks, 128),

time: 34.1 us -> 29.3 us (0.86); the launches traced: 33.6 us -> 29.2 us
  local copies, waits for them, and re-layouts: 4.98 us -> 0.62 us
    unnamed x15 -> x1, local copies, waits for them, and re-layouts: 4.98 us -> 0.62 us
where the time goes in v3:
time: 29.3 us; the launch traced here: 29.2 us
  Pallas kernels  27.9 us (95%)
  between operations  0.66 us (2%)
  local copies, waits for them, and re-layouts  0.62 us (2%)
    pallas_call x1, Pallas kernels, local(): pl.pallas_call(functools.partial(fused_kernel, sizes), out_shape=pltpu.VM...  27.9 us
    unnamed x1, local copies, waits for them, and re-layouts  0.62 us

profile of v3, /device:TPU:0, one launch (start us, length us, event | category | flops | bytes accessed | tf_op | source)
XLA Modules:
  0.0 29.2 jit_solution(2259073111730847104)
XLA Ops:
  0.7 27.9 %shard_map.82 = f32[5,16,128]{2,1,0:T(8,128)S(1)} custom-call(f32[3,16,128]{2,1,0:T(8,128)} %bitcast.13, f32[1,16,128]{2,1,0:T(8,128)} %bitcast.17, s32[8,16]{1,0:T(8,128)} %bitcast.19, s32[1,1]{1,0:T(1,128)} %bitcast.11.count, f32[3,16,128]{2,1,0:T(8,128)} %bitcast.14, f32[16,128]{1,0:T(8,128)} %bitcast.18, f32[2,16,128]{2,1,0:T(8,128)} %bitcast.16, ...), custom_call_target="tpu_custom_call" | custom-call | tf_op jit(solution)/shard_map/pallas_call | solution.py:418
  28.5 0.6 %copy.12 = f32[5,1,1,1,2048]{4,3,2,1,0:T(1,128)} copy(f32[5,1,1,1,2048]{4,3,2,1,0:T(1,128)S(1)} %bitcast.12) | data formatting | bytes 81920

commit v4 on v3

--- a/solution.py
+++ b/solution.py
@@ -51,15 +51,36 @@
     ]
 
 
+def far_first(sizes):
+    nx, ny, _ = sizes
+    turn_x = 2 * lax.rem(lax.axis_index("gx"), 2) - 1
+    turn_y = jnp.where(lax.axis_index("gy") == 0, -1, 1)
+    choices_x = [(1 + turn_x, turn_x), (1 - turn_x, -turn_x)] if nx >= 3 else list(steps_of(nx))
+    choices_y = [(1 + turn_y, turn_y), (1 - turn_y, -turn_y)] if ny >= 3 else list(steps_of(ny))
+    own_x, own_y = (own_kind(nx), 0), (own_kind(ny), 0)
+    order = [(x, y) for y in choices_y for x in choices_x + [own_x]] + [(x, own_y) for x in choices_x]
+    return [((i, j), {"gx": shifted("gx", nx, dx), "gy": shifted("gy", ny, dy)}) for (i, dx), (j, dy) in order]
+
+
+def far_roles(sizes):
+    steps_x, steps_y = len(steps_of(sizes[0])), len(steps_of(sizes[1]))
+    return ([3] * steps_x + [1]) * steps_y + [2] * steps_x
+
+
+def facing_at(kind, count):
+    return 2 - kind if count >= 3 else kind
+
+
 def cores_of(sizes):
     return [(k, {"gz": shifted("gz", sizes[2], dz)}) for k, dz in steps_of(sizes[2])]
 
 
-def greet(sizes):
+def greet(sizes, meanwhile):
     barrier = pltpu.get_barrier_semaphore()
     peers = columns_of(sizes) + cores_of(sizes)
     for _, device in peers:
         pl.semaphore_signal(barrier, inc=1, device_id=device, device_id_type=MESH)
+    meanwhile()
     if peers:
         pl.semaphore_wait(barrier, len(peers))
 
@@ -291,115 +312,146 @@
     rest_in = [pltpu.make_async_copy(src, dst, local_sem.at[2 + n]) for n, (src, dst) in enumerate(pairs)]
     for copy in gas_in + rest_in:
         copy.start()
-    greet(sizes)
-    for copy in gas_in:
-        copy.wait()
-    copies = {}
+
+    def features(i, j, k):
+        for slot, offset in enumerate(offsets()):
+            if place_at(offset, sizes) == place(i, j, k):
+                gas_features([near[place(i, j, k), c] for c in range(4)], feat, slot, offset)
+
+    def meanwhile():
+        for copy in gas_in + rest_in:
+            copy.wait()
+        source_features(pos_v, radius_v, rows, left)
+        one_hots(sizes, tiles, table_v, hot_in, hot_out)
+        spare = jnp.zeros((2 * blocks, 128), jnp.float32)
+        for side in range(2):
+            picked[side, pl.ds(PARTS - 1, 2 * blocks, stride=PARTS), :] = spare
+        features(*own)
+
+    greet(sizes, meanwhile)
     finished = []
 
-    def send(slot, there, device):
-        target = place(*there)
-        copy = pltpu.make_async_remote_copy(
-            src_ref=near.at[place(*slot)],
+    def gas_copy(source, target, device):
+        return pltpu.make_async_remote_copy(
+            src_ref=near.at[source],
             dst_ref=near.at[target],
             send_sem=send_sem.at[target],
             recv_sem=recv_sem.at[target],
             device_id=device,
             device_id_type=MESH,
         )
+
+    def send(source, target, device):
+        copy = gas_copy(source, target, device)
         copy.start()
-        copies[there] = copy
         finished.append(copy)
+
+    def arrived(i, j, k):
+        target = place(i, j, k)
+        gas_copy(target, target, next(iter(cores_of(sizes) + columns_of(sizes)))[1]).wait_recv()
 
     def to_cores(i, j):
         for k, device in cores_of(sizes):
-            send((i, j, own[2]), (i, j, facing(k, nz)), device)
+            send(place(i, j, own[2]), place(i, j, facing(k, nz)), device)
 
     columns = columns_of(sizes)
-    for (i, j), device in columns:
-        send(own, (facing(i, nx), facing(j, ny), own[2]), device)
+    far = far_first(sizes)
+    for (i, j), device in far:
+        send(home, place(facing_at(i, nx), facing_at(j, ny), own[2]), device)
     to_cores(own[0], own[1])
-    for copy in rest_in:
-        copy.wait()
-
-    def features(i, j, k):
-        for slot, offset in enumerate(offsets()):
-            if place_at(offset, sizes) == place(i, j, k):
-                gas_features([near[place(i, j, k), c] for c in range(4)], feat, slot, offset)
-
     def weigh_role(role):
         gather(role, tiles, feat, hot_in, picked)
         weigh(role, picked, left, weights, sums, norms, unroll)
 
-    source_features(pos_v, radius_v, rows, left)
-    one_hots(sizes, tiles, table_v, hot_in, hot_out)
-    spare = jnp.zeros((2 * blocks, 128), jnp.float32)
-    for side in range(2):
-        picked[side, pl.ds(PARTS - 1, 2 * blocks, stride=PARTS), :] = spare
-    features(*own)
     for k, _ in steps_of(nz):
-        copies[own[0], own[1], k].wait_recv()
+        arrived(own[0], own[1], k)
         features(own[0], own[1], k)
     weigh_role(0)
-    across = [at for at, _ in columns if at[0] != own[0]]
-    along = [at for at, _ in columns if at[0] == own[0]]
-    for at in along + across:
-        copies[at[0], at[1], own[2]].wait_recv()
-        to_cores(*at)
-        features(at[0], at[1], own[2])
-    for role in (1, 2, 3):
-        for i, j in along + across:
-            if (i != own[0], j != own[1]) == (role >= 2, role % 2 == 1):
-                for k, _ in steps_of(nz):
-                    copies[i, j, k].wait_recv()
-                    features(i, j, k)
+    def sides(role):
+        return [at for at, _ in columns if 2 * (at[0] != own[0]) + (at[1] != own[1]) == role]
+
+    def take(role):
+        for at in sides(role):
+            arrived(at[0], at[1], own[2])
+            to_cores(*at)
+            pass
+
+    def early(role):
+        for at in sides(role):
+            features(at[0], at[1], own[2])
+
+    def finish(role):
+        for i, j in sides(role):
+            for k, _ in steps_of(nz):
+                arrived(i, j, k)
+                features(i, j, k)
         weigh_role(role)
+
+    take(1)
+    take(2)
+    take(3)
+    early(1)
+    early(2)
+    early(3)
+    finish(1)
+    finish(2)
+    finish(3)
     normalise(count_s, norms, yield_v, momentum_v, loads)
     done = set()
-    along_z, arriving = {}, {}
-
-    def send_gain(src, dst, send_at, recv_at, device):
-        copy = pltpu.make_async_remote_copy(
+
+    def gain_copy(src, dst, send_at, recv_at, device):
+        return pltpu.make_async_remote_copy(
             src_ref=src, dst_ref=dst, send_sem=send_at, recv_sem=recv_at, device_id=device, device_id_type=MESH
         )
+
+    def z_copy(i, j, k, device):
+        at = place(i, j, k)
+        return gain_copy(deposits.at[at], got_z.at[at], gsend_z.at[at], grecv_z.at[at], device)
+
+    def side_copy(i, j, device):
+        at = i * kinds(ny) + j
+        return gain_copy(part.at[at], got.at[at], gsend.at[at], grecv.at[at], device)
+
+    def start(copy):
         copy.start()
         finished.append(copy)
-        return copy
-
-    def role_of(at):
-        return 2 * (at[0] != own[0]) + (at[1] != own[1])
-
-    def send_z(i, j):
+
+    def column_total(i, j):
+        total = deposits[place(i, j, own[2])]
         for k, device in cores_of(sizes):
-            at = place(i, j, k)
-            along_z[i, j, k] = send_gain(deposits.at[at], got_z.at[at], gsend_z.at[at], grecv_z.at[at], device)
+            z_copy(i, j, k, device).wait_recv()
+            total = total + got_z[place(i, j, k)]
+        return total
+
+    def role_columns(role):
+        return [c for c, r in zip(far, far_roles(sizes)) if r == role]
+
+    waiting = []
+
+    def flush():
+        while waiting:
+            start(waiting.pop(0))
+
+    def totals(role):
+        for (i, j), device in role_columns(role):
+            part[i * kinds(ny) + j] = column_total(i, j)
+            flush()
+            waiting.append(side_copy(i, j, device))
 
     for role in (3, 2, 1, 0):
         deposit(role, loads, weights, moved, unroll)
+        flush()
         scatter(role, sizes, hot_out, moved, deposits, done)
-        for i, j in [at for at, _ in columns] + [own[:2]]:
-            if role_of((i, j)) == role:
-                send_z(i, j)
-    ordered = sorted(columns, key=lambda c: -role_of(c[0]))
-
-    def send_part(index):
-        (i, j), device = ordered[index]
-        at = i * kinds(ny) + j
-        arriving[at] = send_gain(part.at[at], got.at[at], gsend.at[at], grecv.at[at], device)
-
-    order = [at for at, _ in ordered] + [own[:2]]
-    for index, (i, j) in enumerate(order):
-        total = deposits[place(i, j, own[2])]
-        for k, _ in steps_of(nz):
-            along_z[i, j, k].wait_recv()
-            total = total + got_z[place(i, j, k)]
-        if index < len(ordered):
-            part[i * kinds(ny) + j] = total
-        if index:
-            send_part(index - 1)
-    for at in reversed(list(arriving)):
-        arriving[at].wait_recv()
-        total = total + got[at]
+        for (i, j), _ in role_columns(role) if role else [(own[:2], None)]:
+            for k, device in cores_of(sizes):
+                start(z_copy(i, j, k, device))
+        if role < 3:
+            totals(role + 1)
+    flush()
+    total = column_total(*own[:2])
+    for (i, j), device in columns:
+        side_copy(i, j, device).wait_recv()
+        total = total + got[i * kinds(ny) + j]
     out[...] = total / near[home, 3]
     for copy in finished:
         copy.wait_send()

time: 29.3 us -> 27.4 us (0.935)
  Pallas kernels: 27.9 us -> 25.9 us
    pallas_call x1, Pallas kernels: 27.9 us -> 25.9 us  [local(): pl.pallas_call(functools.partial(fused_kernel, sizes), out_shape=pltpu.VM...]
where the time goes in v4:
time: 27.4 us; the launch traced here: 27.2 us
  Pallas kernels  25.9 us (95%)
  between operations  0.66 us (2%)
  local copies, waits for them, and re-layouts  0.62 us (2%)
    pallas_call x1, Pallas kernels, local(): pl.pallas_call(functools.partial(fused_kernel, sizes), out_shape=pltpu.VM...  25.9 us
    unnamed x1, local copies, waits for them, and re-layouts  0.62 us

profile of v4, /device:TPU:0, one launch (start us, length us, event | category | flops | bytes accessed | tf_op | source)
XLA Modules:
  0.0 27.2 jit_solution(1688811850858054505)
XLA Ops:
  0.7 25.9 %shard_map.82 = f32[5,16,128]{2,1,0:T(8,128)S(1)} custom-call(f32[3,16,128]{2,1,0:T(8,128)} %bitcast.13, f32[1,16,128]{2,1,0:T(8,128)} %bitcast.17, s32[8,16]{1,0:T(8,128)} %bitcast.19, s32[1,1]{1,0:T(1,128)} %bitcast.11.count, f32[3,16,128]{2,1,0:T(8,128)} %bitcast.14, f32[16,128]{1,0:T(8,128)} %bitcast.18, f32[2,16,128]{2,1,0:T(8,128)} %bitcast.16, ...), custom_call_target="tpu_custom_call" | custom-call | tf_op jit(solution)/shard_map/pallas_call | solution.py:470
  26.6 0.6 %copy.12 = f32[5,1,1,1,2048]{4,3,2,1,0:T(1,128)} copy(f32[5,1,1,1,2048]{4,3,2,1,0:T(1,128)S(1)} %bitcast.12) | data formatting | bytes 81920

commit v5 on v4

--- a/solution.py
+++ b/solution.py
@@ -77,7 +77,8 @@
 
 def greet(sizes, meanwhile):
     barrier = pltpu.get_barrier_semaphore()
-    peers = columns_of(sizes) + cores_of(sizes)
+    own = (own_kind(sizes[0]), own_kind(sizes[1]))
+    peers = [c for c in columns_of(sizes) if c[0][0] == own[0] or c[0][1] == own[1]] + cores_of(sizes)
     for _, device in peers:
         pl.semaphore_signal(barrier, inc=1, device_id=device, device_id_type=MESH)
     meanwhile()
@@ -169,7 +170,7 @@
     pairs = hot_in.shape[1]
     got = jnp.dot(hot_in[role, :, 0:depth], feat[first : first + depth, :], preferred_element_type=jnp.float32)
     for row in range(PARTS - 1):
-        picked[role % 2, pl.ds(row, pairs, stride=PARTS), :] = got[:, row * 128 : row * 128 + 128]
+        picked[role, pl.ds(row, pairs, stride=PARTS), :] = got[:, row * 128 : row * 128 + 128]
 
 
 def weigh(role, picked, left, weights, sums, norms, unroll):
@@ -179,7 +180,7 @@
         near = []
         for z in range(2):
             at = pl.multiple_of((z * blocks + b) * PARTS, PARTS)
-            near.append(picked[role % 2, pl.ds(at, PARTS), :].astype(jnp.bfloat16))
+            near.append(picked[role, pl.ds(at, PARTS), :].astype(jnp.bfloat16))
         rhs = jnp.concatenate([jnp.concatenate(near, axis=1)] * 3, axis=0)
         u = jnp.dot(left[b], rhs, preferred_element_type=jnp.float32)
         w = 1.0 / (u * u)
@@ -285,14 +286,14 @@
         pltpu.VMEM((4, blocks * 16, 128), jnp.float32),
         pltpu.VMEM((4, 2 * blocks, 12 * tiles), jnp.bfloat16),
         pltpu.VMEM((4, 12 * tiles, 4 * blocks), jnp.bfloat16),
-        pltpu.VMEM((2, 2 * blocks * PARTS, 128), jnp.float32),
+        pltpu.VMEM((4, 2 * blocks * PARTS, 128), jnp.float32),
     ]
 
 
 def fused_kernel(sizes, pos, mass, table, count, spos, sradius, syield, smomentum, out, *scratch):
     (near, count_s, table_v, pos_v, radius_v, yield_v, momentum_v, deposits, part, got_z, got) = scratch[:11]
     (feat, rows, left, weights, sums, norms, loads, moved, hot_in, hot_out, picked) = scratch[11:22]
-    local_sem, send_sem, recv_sem, gsend_z, grecv_z, gsend, grecv = scratch[22:]
+    local_sem, send_sem, recv_sem, gsend_z, grecv_z, gsend, grecv, ready_sem = scratch[22:]
     nx, ny, nz = sizes
     own = tuple(own_kind(n) for n in sizes)
     tiles = near.shape[2]
@@ -324,7 +325,7 @@
         source_features(pos_v, radius_v, rows, left)
         one_hots(sizes, tiles, table_v, hot_in, hot_out)
         spare = jnp.zeros((2 * blocks, 128), jnp.float32)
-        for side in range(2):
+        for side in range(4):
             picked[side, pl.ds(PARTS - 1, 2 * blocks, stride=PARTS), :] = spare
         features(*own)
 
@@ -355,18 +356,30 @@
             send(place(i, j, own[2]), place(i, j, facing(k, nz)), device)
 
     columns = columns_of(sizes)
-    far = far_first(sizes)
-    for (i, j), device in far:
-        send(home, place(facing_at(i, nx), facing_at(j, ny), own[2]), device)
+    far = list(zip(far_first(sizes), far_roles(sizes)))
+    others = [device for at, device in columns if at[0] != own[0] and at[1] == own[1]]
+    corners = [device for at, device in columns if at[0] != own[0] and at[1] != own[1]]
+    if corners:
+        for device in others:
+            pl.semaphore_signal(ready_sem, inc=1, device_id=device, device_id_type=MESH)
+
+    def send_home(roles):
+        for ((i, j), device), role in far:
+            if role in roles:
+                send(home, place(facing_at(i, nx), facing_at(j, ny), own[2]), device)
+
+    def ready():
+        if corners:
+            pl.semaphore_wait(ready_sem, len(others))
+        send_home((3,))
+
+    send_home((1, 2))
     to_cores(own[0], own[1])
+
     def weigh_role(role):
         gather(role, tiles, feat, hot_in, picked)
         weigh(role, picked, left, weights, sums, norms, unroll)
 
-    for k, _ in steps_of(nz):
-        arrived(own[0], own[1], k)
-        features(own[0], own[1], k)
-    weigh_role(0)
     def sides(role):
         return [at for at, _ in columns if 2 * (at[0] != own[0]) + (at[1] != own[1]) == role]
 
@@ -387,15 +400,39 @@
                 features(i, j, k)
         weigh_role(role)
 
+    def received(role):
+        for i, j in sides(role):
+            for k, _ in steps_of(nz):
+                arrived(i, j, k)
+                features(i, j, k)
+
+    def pick(role):
+        gather(role, tiles, feat, hot_in, picked)
+
+    def weight(role):
+        weigh(role, picked, left, weights, sums, norms, unroll)
+
+    ready()
+    for k, _ in steps_of(nz):
+        arrived(own[0], own[1], k)
+        features(own[0], own[1], k)
+    pick(0)
+    weight(0)
     take(1)
     take(2)
-    take(3)
     early(1)
     early(2)
+    received(1)
+    pick(1)
+    received(2)
+    pick(2)
+    weight(1)
+    weight(2)
+    take(3)
     early(3)
-    finish(1)
-    finish(2)
-    finish(3)
+    received(3)
+    pick(3)
+    weight(3)
     normalise(count_s, norms, yield_v, momentum_v, loads)
     done = set()
 
@@ -424,7 +461,7 @@
         return total
 
     def role_columns(role):
-        return [c for c, r in zip(far, far_roles(sizes)) if r == role]
+        return [c for c, r in far if r == role]
 
     waiting = []
 
@@ -492,6 +529,7 @@
             dma((slots,)),
             dma((sides,)),
             dma((sides,)),
+            pltpu.SemaphoreType.REGULAR,
         ],
         compiler_params=pltpu.CompilerParams(collective_id=0, has_side_effects=True, vmem_limit_bytes=LIMIT),
     )(

time: 27.4 us -> 25.9 us (0.945)
  Pallas kernels: 25.9 us -> 24.5 us
    pallas_call x1, Pallas kernels: 25.9 us -> 24.5 us  [local(): pl.pallas_call(functools.partial(fused_kernel, sizes), out_shape=pltpu.VM...]
where the time goes in v5:
time: 25.9 us; the launch traced here: 25.8 us
  Pallas kernels  24.5 us (95%)
  between operations  0.66 us (3%)
  local copies, waits for them, and re-layouts  0.62 us (2%)
    pallas_call x1, Pallas kernels, local(): pl.pallas_call(functools.partial(fused_kernel, sizes), out_shape=pltpu.VM...  24.5 us
    unnamed x1, local copies, waits for them, and re-layouts  0.62 us

profile of v5, /device:TPU:0, one launch (start us, length us, event | category | flops | bytes accessed | tf_op | source)
XLA Modules:
  0.0 25.8 jit_solution(11539852486558098133)
XLA Ops:
  0.7 24.5 %shard_map.82 = f32[5,16,128]{2,1,0:T(8,128)S(1)} custom-call(f32[3,16,128]{2,1,0:T(8,128)} %bitcast.13, f32[1,16,128]{2,1,0:T(8,128)} %bitcast.17, s32[8,16]{1,0:T(8,128)} %bitcast.19, s32[1,1]{1,0:T(1,128)} %bitcast.11.count, f32[3,16,128]{2,1,0:T(8,128)} %bitcast.14, f32[16,128]{1,0:T(8,128)} %bitcast.18, f32[2,16,128]{2,1,0:T(8,128)} %bitcast.16, ...), custom_call_target="tpu_custom_call" | custom-call | tf_op jit(solution)/shard_map/pallas_call | solution.py:507
  25.1 0.6 %copy.12 = f32[5,1,1,1,2048]{4,3,2,1,0:T(1,128)} copy(f32[5,1,1,1,2048]{4,3,2,1,0:T(1,128)S(1)} %bitcast.12) | data formatting | bytes 81920

commit v6 on v5

--- a/solution.py
+++ b/solution.py
@@ -203,8 +203,7 @@
     lane = lax.broadcasted_iota(jnp.int32, (blocks, 128), 1)
     index = lax.broadcasted_iota(jnp.int32, (blocks, 128), 0) * 128 + lane
     scale = jnp.where(index < count[0, 0], 1.0, 0.0) / norms[...]
-    zero = jnp.zeros_like(scale)
-    for q, value in enumerate([yields[0], momentum[0], momentum[1], momentum[2], yields[1], zero, zero, zero]):
+    for q, value in enumerate([yields[0], momentum[0], momentum[1], momentum[2], yields[1]]):
         coef = value * scale
         high = coef.astype(jnp.bfloat16).astype(jnp.float32)
         loads[pl.ds(q, blocks, stride=16), :] = high
@@ -315,15 +314,17 @@
         copy.start()
 
     def features(i, j, k):
+        gas = [near[place(i, j, k), c] for c in range(4)]
         for slot, offset in enumerate(offsets()):
             if place_at(offset, sizes) == place(i, j, k):
-                gas_features([near[place(i, j, k), c] for c in range(4)], feat, slot, offset)
+                gas_features(gas, feat, slot, offset)
 
     def meanwhile():
         for copy in gas_in + rest_in:
             copy.wait()
         source_features(pos_v, radius_v, rows, left)
         one_hots(sizes, tiles, table_v, hot_in, hot_out)
+        loads[...] = jnp.zeros_like(loads)
         spare = jnp.zeros((2 * blocks, 128), jnp.float32)
         for side in range(4):
             picked[side, pl.ds(PARTS - 1, 2 * blocks, stride=PARTS), :] = spare

time: 25.9 us -> 25.9 us (level)
  no operation moved by 1% of the time
where the time goes in v6:
time: 25.9 us; the launch traced here: 25.7 us
  Pallas kernels  24.5 us (95%)
  between operations  0.66 us (3%)
  local copies, waits for them, and re-layouts  0.62 us (2%)
    pallas_call x1, Pallas kernels, local(): pl.pallas_call(functools.partial(fused_kernel, sizes), out_shape=pltpu.VM...  24.5 us
    unnamed x1, local copies, waits for them, and re-layouts  0.62 us

profile of v6, /device:TPU:0, one launch (start us, length us, event | category | flops | bytes accessed | tf_op | source)
XLA Modules:
  0.0 25.7 jit_solution(17535613443288599555)
XLA Ops:
  0.7 24.5 %shard_map.82 = f32[5,16,128]{2,1,0:T(8,128)S(1)} custom-call(f32[3,16,128]{2,1,0:T(8,128)} %bitcast.13, f32[1,16,128]{2,1,0:T(8,128)} %bitcast.17, s32[8,16]{1,0:T(8,128)} %bitcast.19, s32[1,1]{1,0:T(1,128)} %bitcast.11.count, f32[3,16,128]{2,1,0:T(8,128)} %bitcast.14, f32[16,128]{1,0:T(8,128)} %bitcast.18, f32[2,16,128]{2,1,0:T(8,128)} %bitcast.16, ...), custom_call_target="tpu_custom_call" | custom-call | tf_op jit(solution)/shard_map/pallas_call | solution.py:508
  25.1 0.6 %copy.12 = f32[5,1,1,1,2048]{4,3,2,1,0:T(1,128)} copy(f32[5,1,1,1,2048]{4,3,2,1,0:T(1,128)S(1)} %bitcast.12) | data formatting | bytes 81920
